TPU v7x, 256 devices: a whole 4x4x8 slice. The times are simulated.
256 devices in a mesh: dp: 8 (over z), section: 2 (over core), space: 16 (over y, x).
Axes of the slice: x: 4, y: 4, z: 8, core: 2. Of those that a mesh axis runs over, the one named last changes fastest.
Arguments:
- latents: bfloat16 [32, 96, 192, 320], P('dp', 'space'), parts along dimension 0, may hold values from -16 to 16
- kernels: bfloat16 [2, 3, 3, 320, 320], P('section'), may hold values from -0.109375 to 0.109375
- norm_gain: float32 [2, 320], P('section'), may hold values from 0.25 to 1.75
- norm_bias: float32 [2, 320], P('section'), may hold values from -3 to 3
- conv_bias: float32 [2, 320], P('section'), may hold values from -3 to 3
Outputs:
- skips: bfloat16 [2, 32, 96, 192, 320], P('section', 'dp', 'space'), parts along dimension 1
There are 8 independent parts, one for each index of `dp`. A program takes and returns all parts, laid end to end along the dimension named above; an argument that names none is the same for every part. Nothing has to cross between parts.
All inputs are finite; a program needn't handle non-finite values.
Results may differ from a plain program's by a relative error of at most 0.01.
Values may be sent and summed in bfloat16 or wider, within the bound.
A program may use at most 128 MiB of HBM per device.

v0:
```python
import jax
import jax.numpy as jnp
from jax import lax
from jax.sharding import PartitionSpec as P

GROUPS = 32


def sent_to_all(array, axis):
    copies = jnp.broadcast_to(array, (lax.axis_size(axis), *array.shape))
    return lax.all_to_all(copies, axis, split_axis=0, concat_axis=0, tiled=True)


def of_everyone(array, axis):
    return sent_to_all(array, axis).sum(axis=0)


def together(arrays, axis):
    flat, at, gathered = (jnp.concatenate([a.reshape(-1) for a in arrays]), 0, [])
    total = of_everyone(flat, axis)
    for a in arrays:
        gathered.append(total[at : at + a.size].reshape(a.shape))
        at += a.size
    return tuple(gathered)


def padded_2(array, sides, width):
    for axis, dim in sides:
        size, length = (lax.axis_size(axis), array.shape[dim])
        up = [(i, (i + 1) % size) for i in range(size - 1)]
        down = [(j, i) for i, j in up]
        last = lax.slice_in_dim(array, length - width, length, axis=dim)
        initial = lax.slice_in_dim(array, 0, width, axis=dim)
        before = lax.ppermute(last, axis, up)
        after = lax.ppermute(initial, axis, down)
        array = jnp.concatenate([before, array, after], axis=dim)
    return array


def group_moments(inputs):
    batch_count, local_rows, columns, channels = inputs.shape
    members = local_rows * lax.axis_size("space") * columns * (channels // GROUPS)
    values = inputs.astype(jnp.float32).reshape(
        batch_count, local_rows * columns, GROUPS, channels // GROUPS
    )
    totals, squares = together(
        (jnp.sum(values, axis=(1, 3)), jnp.sum(values * values, axis=(1, 3))), "space"
    )
    group_mean = totals / members
    group_var = jnp.maximum(squares / members - group_mean * group_mean, 0.0)
    return (group_mean, lax.rsqrt(group_var + 1e-05))


def apply_layer(inputs, kernel, norm_gain, norm_shift, shift_bias, residual):
    batch_count, local_rows, columns, channels = inputs.shape
    group_mean, inv_spread = group_moments(inputs)
    padded = padded_2(inputs, (("space", 1),), 1)
    values = padded.astype(jnp.float32).reshape(
        batch_count, local_rows + 2, columns, GROUPS, channels // GROUPS
    )
    scaled = (values - group_mean[:, None, None, :, None]) * inv_spread[:, None, None, :, None]
    scaled = scaled.reshape(batch_count, local_rows + 2, columns, channels) * norm_gain + norm_shift
    activated = jax.nn.silu(scaled)
    space_index = lax.axis_index("space")
    row_place = lax.broadcasted_iota(jnp.int32, (1, local_rows + 2, 1, 1), 1)
    outside = jnp.logical_or(
        jnp.logical_and(space_index == 0, row_place == 0),
        jnp.logical_and(space_index == lax.axis_size("space") - 1, row_place == local_rows + 1),
    )
    normed = jnp.where(outside, 0.0, activated).astype(jnp.bfloat16)
    convolved = lax.conv_general_dilated(
        normed,
        kernel,
        (1, 1),
        ((0, 0), (1, 1)),
        dimension_numbers=("NHWC", "HWIO", "NHWC"),
        preferred_element_type=jnp.float32,
    )
    return (residual + convolved + shift_bias).astype(jnp.bfloat16)


def on_device(latents, kernels, norm_gain, norm_bias, conv_bias):
    section_count = lax.axis_size("section")
    section_index = lax.axis_index("section")
    sample_count = latents.shape[0]
    per_section = sample_count // section_count
    own = lax.dynamic_slice_in_dim(latents, section_index * per_section, per_section, 0)
    all_kernels, all_gains, all_shifts, all_biases = (
        lax.all_gather(kernels, "section", axis=0, tiled=True),
        lax.all_gather(norm_gain.astype(jnp.bfloat16), "section", axis=0, tiled=True).astype(
            norm_gain.dtype
        ),
        lax.all_gather(norm_bias.astype(jnp.bfloat16), "section", axis=0, tiled=True).astype(
            norm_bias.dtype
        ),
        lax.all_gather(conv_bias.astype(jnp.bfloat16), "section", axis=0, tiled=True).astype(
            conv_bias.dtype
        ),
    )
    first = apply_layer(
        own,
        all_kernels[0],
        all_gains[0],
        all_shifts[0],
        all_biases[0],
        jnp.zeros(own.shape, jnp.float32),
    )
    second = apply_layer(
        first, all_kernels[1], all_gains[1], all_shifts[1], all_biases[1], own.astype(jnp.float32)
    )
    stacked = jnp.stack([first, second])
    return lax.all_to_all(stacked, "section", split_axis=0, concat_axis=1, tiled=True)


def solution(mesh):
    return jax.shard_map(
        on_device,
        mesh=mesh,
        in_specs=(
            P("dp", "space", None, None),
            P("section", None, None, None, None),
            P("section", None),
            P("section", None),
            P("section", None),
        ),
        out_specs=P("section", "dp", "space", None, None),
        check_vma=False,
    )
```

profile of v0, /device:TPU:1, one launch (start us, length us, event | category | flops | bytes accessed | tf_op | source)
XLA Modules:
  0.0 147.8 jit_solution(6580711174692724752)
XLA Ops:
  10.0 1.4 convert_reduce_fusion
  12.7 7.6 %all-to-all-start = ((f32[16,1,128]{2,1,0:T(1,128)}), f32[16,1,128]{2,1,0:T(1,128)S(1)}, u32[]{:S(2)}, u32[]{:S(2)}) async-start(f32[16,1,128]{2,1,0:T(1,128)} %broadcast_in_dim.28), calls=%async_computation | async-start | bytes 16384 | tf_op jit(solution)/shard_map/all_to_all | solution.py:11
  20.3 2.6 %copy.102 = bf16[2,6,192,320]{3,1,2,0:T(8,128)(2,1)S(1)} copy(bf16[2,6,192,320]{3,2,1,0:T(8,128)(2,1)} %copy-done.2) | data formatting | bytes 2949120
  24.4 3.3 %collective-permute-start = (bf16[2,1,192,320]{3,2,1,0:T(8,128)(2,1)}, bf16[2,1,192,320]{3,2,1,0:T(8,128)(2,1)S(1)}, u32[]{:S(2)}, u32[]{:S(2)}) collective-permute-start(bf16[2,1,192,320]{3,2,1,0:T(8,128)(2,1)} %copy.77), channel_id=1, source_target_pairs={{0,1},{1,2},{2,3},{3,4},{4,5},{5,6},{6,7},{7,8},{8,9},{9,10},{10,1... | collective-permute-start | bytes 737288 | tf_op jit(solution)/shard_map/ppermute | solution.py:34
  27.8 1.3 collective-permute-start.1
  29.1 3.0 %all-gather = bf16[2,1,320]{2,1,0:T(2,128)(2,1)S(1)} all-gather(bf16[1,1,320]{2,1,0:T(2,128)(2,1)S(1)} %convert_bitcast_fusion.2), channel_id=1, replica_groups=mesh['dp'=8,'section'=2,'space'=16] {'section'}, dimensions={0}, use_global_device_ids=true | all-gather | bytes 1920 | tf_op jit(solution)/shard_map/all_gather | solution.py:90
  32.1 1.9 %all-gather.1 = bf16[2,1,320]{2,1,0:T(2,128)(2,1)S(1)} all-gather(bf16[1,1,320]{2,1,0:T(2,128)(2,1)S(1)} %convert_bitcast_fusion.1), channel_id=1, replica_groups=mesh['dp'=8,'section'=2,'space'=16] {'section'}, dimensions={0}, use_global_device_ids=true | all-gather | bytes 1920 | tf_op jit(solution)/shard_map/all_gather | solution.py:93
  34.7 2.0 %all-gather.2 = bf16[2,1,320]{2,1,0:T(2,128)(2,1)S(1)} all-gather(bf16[1,1,320]{2,1,0:T(2,128)(2,1)S(1)} %convert_bitcast_fusion), channel_id=1, replica_groups=mesh['dp'=8,'section'=2,'space'=16] {'section'}, dimensions={0}, use_global_device_ids=true | all-gather | bytes 1920 | tf_op jit(solution)/shard_map/all_gather | solution.py:96
  40.2 1.4 copy.80
  41.6 4.4 %fusion.13 = bf16[8,2,192,320]{3,0,2,1:T(8,128)(2,1)S(1)} fusion(bf16[2,1,192,320]{3,1,2,0:T(2,128)(2,1)S(1)} %copy.80, bf16[2,6,192,320]{3,1,2,0:T(8,128)(2,1)S(1)} %copy.102, bf16[2,1,192,320]{3,1,2,0:T(2,128)(2,1)S(1)} %copy.79, f32[320]{0:T(512)} %get-tuple-element.12, f32[320]{0:T(512)} %get-tuple-element.10, f32[2,320]{1,0:T(2,128)S(1)} %mul.82, ...), kind=kLoop, calls=%fused_computation.24 | loop fusion | flops 15728640 | bytes 3939848 | tf_op jit(solution)/shard_map/convert_element_type | solution.py:70
  46.3 1.8 %fusion.5 = bf16[8,2,8,27,320]{4,0,3,2,1:T(8,128)(2,1)} fusion(bf16[8,2,7,2,320]{4,0,3,2,1:T(8,128)(2,1)S(1)} %slice.120, bf16[8,2,8,25,320]{4,0,3,2,1:T(8,128)(2,1)S(1)} %bitcast.67), kind=kLoop, calls=%fused_computation.16 | loop fusion | flops 6635520 | bytes 4403200 | tf_op jit(solution)/shard_map/conv_general_dilated | solution.py:71
  48.1 11.4 %convert_multiply_fusion.1 = (f32[6,16,25,320]{3,1,2,0:T(8,128)}, bf16[6,16,25,320]{3,1,2,0:T(8,128)(2,1)S(1)}) fusion(f32[320]{0:T(512)S(1)} %copy-done.7, bf16[2,3,3,320,320]{4,3,2,1,0:T(8,128)(2,1)} %all-gather.5.cloned.1.call-done, bf16[8,2,8,27,320]{4,0,3,2,1:T(8,128)(2,1)} %fusion.5, pred[16,25]{0,1:T(8,128)(4,1)S(1)} %copy-done.10), kind=kOutput, calls=%fused_computation.32 | convolution fusion | flops 4427520000 | bytes 9475728 | tf_op jit(solution)/shard_map/conv_general_dilated | solution.py:71
  59.5 2.8 %copy.91 = f32[6,16,25,320]{3,2,1,0:T(8,128)} copy(bf16[6,16,25,320]{3,1,2,0:T(8,128)(2,1)S(1)} %get-tuple-element.24) | data formatting | bytes 4608000 | tf_op jit(solution)/shard_map/convert_element_type | solution.py:43
  62.3 2.0 %copy.98 = bf16[6,16,25,320]{3,0,2,1:T(8,128)(2,1)} copy(bf16[6,16,25,320]{3,1,2,0:T(8,128)(2,1)S(1)} %get-tuple-element.24) | data formatting | bytes 3072000 | tf_op jit(solution)/shard_map/convert_element_type | solution.py:79
  64.3 4.8 %reshape.176 = f32[6,2,200,320]{3,2,1,0:T(8,128)} reshape(f32[6,16,25,320]{3,2,1,0:T(8,128)} %copy.91) | data formatting | bytes 6144000 | tf_op jit(solution)/shard_map/convert_element_type | solution.py:43
  69.1 2.3 %slice_reduce_fusion.1 = f32[2,320]{1,0:T(2,128)S(1)} fusion(f32[6,2,200,320]{3,2,1,0:T(8,128)} %reshape.176), kind=kLoop, calls=%fused_computation.15 | loop fusion | flops 736640 | bytes 2951680 | tf_op jit(solution)/shard_map/reduce_sum | solution.py:47
  71.7 5.4 %copy.92 = f32[6,16,25,320]{3,2,1,0:T(8,128)} copy(f32[6,16,25,320]{3,1,2,0:T(8,128)} %get-tuple-element.23) | data formatting | bytes 6144000 | tf_op jit(solution)/shard_map/mul | solution.py:47
  77.1 4.8 %reshape.178 = f32[6,2,200,320]{3,2,1,0:T(8,128)} reshape(f32[6,16,25,320]{3,2,1,0:T(8,128)} %copy.92) | data formatting | bytes 6144000 | tf_op jit(solution)/shard_map/mul | solution.py:47
  81.9 2.4 %slice_reduce_fusion = f32[2,320]{1,0:T(2,128)S(1)} fusion(f32[6,2,200,320]{3,2,1,0:T(8,128)} %reshape.178), kind=kLoop, calls=%fused_computation.14 | loop fusion | flops 736640 | bytes 2951680 | tf_op jit(solution)/shard_map/reduce_sum | solution.py:47
  85.3 7.7 %all-to-all-start.1 = ((f32[16,1,128]{2,1,0:T(1,128)}), f32[16,1,128]{2,1,0:T(1,128)S(1)}, u32[]{:S(2)}, u32[]{:S(2)}) async-start(f32[16,1,128]{2,1,0:T(1,128)} %broadcast_in_dim.29), calls=%async_computation.1 | async-start | bytes 16384 | tf_op jit(solution)/shard_map/all_to_all | solution.py:11
  93.0 2.6 %slice_bitcast_fusion.5 = (bf16[1,2,6,192,320]{4,2,3,1,0:T(8,128)(2,1)}, bf16[2,6,192,320]{3,1,2,0:T(8,128)(2,1)}) fusion(bf16[6,2,200,320]{3,0,2,1:T(8,128)(2,1)S(1)} %bitcast.68), kind=kLoop, calls=%fused_computation.29 | loop fusion | bytes 4423680 | tf_op jit(solution)/shard_map/stack | solution.py:111
  96.6 3.5 %collective-permute-start.2 = (bf16[2,1,192,320]{3,2,1,0:T(8,128)(2,1)}, bf16[2,1,192,320]{3,2,1,0:T(8,128)(2,1)S(1)}, u32[]{:S(2)}, u32[]{:S(2)}) collective-permute-start(bf16[2,1,192,320]{3,2,1,0:T(8,128)(2,1)} %slice_bitcast_fusion.12), channel_id=1, source_target_pairs={{0,1},{1,2},{2,3},{3,4},{4,5},{5,6},{6,7},{7,8},{8,9},{9,10},{10,1... | collective-permute-start | bytes 737288 | tf_op jit(solution)/shard_map/ppermute | solution.py:34
  101.1 1.3 collective-permute-start.3
  103.1 2.6 %collective-permute-done.2 = bf16[2,1,192,320]{3,2,1,0:T(8,128)(2,1)S(1)} collective-permute-done((bf16[2,1,192,320]{3,2,1,0:T(8,128)(2,1)}, bf16[2,1,192,320]{3,2,1,0:T(8,128)(2,1)S(1)}, u32[]{:S(2)}, u32[]{:S(2)}) %collective-permute-start.2) | collective-permute-done | bytes 245792 | tf_op jit(solution)/shard_map/ppermute | solution.py:34
  106.1 4.6 %collective-permute-done.3 = bf16[2,1,192,320]{3,2,1,0:T(8,128)(2,1)} collective-permute-done((bf16[2,1,192,320]{3,2,1,0:T(8,128)(2,1)}, bf16[2,1,192,320]{3,2,1,0:T(8,128)(2,1)}, u32[]{:S(2)}, u32[]{:S(2)}) %collective-permute-start.3) | collective-permute-done | bytes 245792 | tf_op jit(solution)/shard_map/ppermute | solution.py:35
  110.7 1.4 copy.90
  112.2 4.5 %fusion.14 = bf16[8,2,192,320]{3,0,2,1:T(8,128)(2,1)S(1)} fusion(bf16[2,1,192,320]{3,1,2,0:T(2,128)(2,1)S(1)} %copy.90, bf16[2,6,192,320]{3,1,2,0:T(8,128)(2,1)S(1)} %copy-done.6, bf16[2,1,192,320]{3,1,2,0:T(2,128)(2,1)S(1)} %copy.89, f32[320]{0:T(512)} %get-tuple-element.11, f32[320]{0:T(512)S(1)} %get-tuple-element.9, f32[2,320]{1,0:T(2,128)S(1)} %mul.92, ...), kind=kLoop, calls=%fused_computation.25 | loop fusion | flops 15728640 | bytes 3939848 | tf_op jit(solution)/shard_map/convert_element_type | solution.py:70
  117.7 7.7 %broadcast_select_fusion = f32[6,16,25,320]{3,1,2,0:T(8,128)S(1)} fusion(pred[16,25]{0,1:T(8,128)(4,1)S(1)} %copy-done.11, bf16[2,3,3,320,320]{4,3,2,1,0:T(8,128)(2,1)S(1)} %bitcast.72, bf16[8,2,8,27,320]{4,0,3,2,1:T(8,128)(2,1)S(1)} %fusion.6), kind=kOutput, calls=%fused_computation.31 | convolution fusion | flops 4424448000 | bytes 7942144 | tf_op jit(solution)/shard_map/conv_general_dilated | solution.py:71
  126.9 1.6 %fusion.15 = bf16[1,2,6,192,320]{4,2,3,1,0:T(8,128)(2,1)S(1)} fusion(f32[6,2,200,320]{3,0,2,1:T(8,128)S(1)} %bitcast.62, f32[320]{0:T(512)S(1)} %get-tuple-element.7, bf16[2,6,192,320]{3,2,1,0:T(8,128)(2,1)S(1)} %copy-done.3), kind=kLoop, calls=%fused_computation.26 | loop fusion | flops 2949120 | bytes 5899520 | tf_op jit(solution)/shard_map/stack | solution.py:111
  128.5 1.4 pad_maximum_fusion
  130.6 8.5 %all_to_all.24 = bf16[2,2,6,192,320]{4,3,2,1,0:T(8,128)(2,1)S(1)} all-to-all(bf16[2,2,6,192,320]{4,3,2,1,0:T(8,128)(2,1)S(1)} %copy.97), channel_id=1, replica_groups=mesh['dp'=8,'section'=2,'space'=16] {'section'}, dimensions={0} | all-to-all | bytes 5898240 | tf_op jit(solution)/shard_map/all_to_all | solution.py:112
  139.1 1.8 %copy.121 = bf16[1,4,6,192,320]{4,3,2,1,0:T(8,128)(2,1)} copy(bf16[1,4,6,192,320]{4,3,2,1,0:T(8,128)(2,1)S(1)} %bitcast.63) | data formatting | bytes 5898240
  (100 shorter events, 18.3 us)
Async XLA Ops:
  6.5 2.0 %copy-start = (bf16[4,6,192,320]{3,2,1,0:T(8,128)(2,1)S(1)}, bf16[4,6,192,320]{3,2,1,0:T(8,128)(2,1)}, u32[]{:S(2)}) copy-start(bf16[4,6,192,320]{3,2,1,0:T(8,128)(2,1)} %param.5) | copy-start | bytes 8847364
  6.5 41.6 %all-gather.5.cloned.1.call-start = ((), (), s32[]{:S(2)}) async-start(), calls=%async_computation.3 | async-start | bytes 6635520 | tf_op jit(solution)/shard_map/all_gather | solution.py:89
  8.7 1.2 copy-start.2
  12.7 26.4 %all-to-all-start = ((f32[16,1,128]{2,1,0:T(1,128)}), f32[16,1,128]{2,1,0:T(1,128)S(1)}, u32[]{:S(2)}, u32[]{:S(2)}) async-start(f32[16,1,128]{2,1,0:T(1,128)} %broadcast_in_dim.28), calls=%async_computation | async-start | bytes 16384 | tf_op jit(solution)/shard_map/all_to_all | solution.py:11
  20.2 8.8 %copy-start.8 = (f32[1,320]{1,0:T(1,128)S(1)}, f32[1,320]{1,0:T(1,128)}, u32[]{:S(2)}) copy-start(f32[1,320]{1,0:T(1,128)} %param.7) | copy-start | bytes 3844
  20.3 11.9 %copy-start.9 = (f32[1,320]{1,0:T(1,128)S(1)}, f32[1,320]{1,0:T(1,128)}, u32[]{:S(2)}) copy-start(f32[1,320]{1,0:T(1,128)} %param.8) | copy-start | bytes 3844
  24.4 15.3 %collective-permute-start = (bf16[2,1,192,320]{3,2,1,0:T(8,128)(2,1)}, bf16[2,1,192,320]{3,2,1,0:T(8,128)(2,1)S(1)}, u32[]{:S(2)}, u32[]{:S(2)}) collective-permute-start(bf16[2,1,192,320]{3,2,1,0:T(8,128)(2,1)} %copy.77), channel_id=1, source_target_pairs={{0,1},{1,2},{2,3},{3,4},{4,5},{5,6},{6,7},{7,8},{8,9},{9,10},{10,1... | collective-permute-start | bytes 737288 | tf_op jit(solution)/shard_map/ppermute | solution.py:34
  27.8 12.4 %collective-permute-start.1 = (bf16[2,1,192,320]{3,2,1,0:T(8,128)(2,1)S(1)}, bf16[2,1,192,320]{3,2,1,0:T(8,128)(2,1)}, u32[]{:S(2)}, u32[]{:S(2)}) collective-permute-start(bf16[2,1,192,320]{3,2,1,0:T(8,128)(2,1)S(1)} %copy.78), channel_id=1, source_target_pairs={{1,0},{2,1},{3,2},{4,3},{5,4},{6,5},{7,6},{8,7},{9,8},{10,9},{11,1... | collective-permute-start | bytes 737288 | tf_op jit(solution)/shard_map/ppermute | solution.py:35
  46.3 1.8 %copy-start.7 = (f32[320]{0:T(512)S(1)}, f32[320]{0:T(512)}, u32[]{:S(2)}) copy-start(f32[320]{0:T(512)} %get-tuple-element.8) | copy-start | bytes 3844
  46.3 1.8 %copy-start.10 = (pred[16,25]{0,1:T(8,128)(4,1)S(1)}, pred[16,25]{0,1:T(8,128)(4,1)}, u32[]{:S(2)}) copy-start(pred[16,25]{0,1:T(8,128)(4,1)} %constant.48) | copy-start | bytes 1204
  81.9 11.1 %copy-start.4 = (bf16[6,16,25,320]{3,0,2,1:T(8,128)(2,1)S(1)}, bf16[6,16,25,320]{3,0,2,1:T(8,128)(2,1)}, u32[]{:S(2)}) copy-start(bf16[6,16,25,320]{3,0,2,1:T(8,128)(2,1)} %copy.98) | copy-start | bytes 4608004
  85.3 17.1 %all-to-all-start.1 = ((f32[16,1,128]{2,1,0:T(1,128)}), f32[16,1,128]{2,1,0:T(1,128)S(1)}, u32[]{:S(2)}, u32[]{:S(2)}) async-start(f32[16,1,128]{2,1,0:T(1,128)} %broadcast_in_dim.29), calls=%async_computation.1 | async-start | bytes 16384 | tf_op jit(solution)/shard_map/all_to_all | solution.py:11
  95.6 16.5 %copy-start.6 = (bf16[2,6,192,320]{3,1,2,0:T(8,128)(2,1)S(1)}, bf16[2,6,192,320]{3,1,2,0:T(8,128)(2,1)}, u32[]{:S(2)}) copy-start(bf16[2,6,192,320]{3,1,2,0:T(8,128)(2,1)} %get-tuple-element.14) | copy-start | bytes 4423684
  96.6 9.0 %collective-permute-start.2 = (bf16[2,1,192,320]{3,2,1,0:T(8,128)(2,1)}, bf16[2,1,192,320]{3,2,1,0:T(8,128)(2,1)S(1)}, u32[]{:S(2)}, u32[]{:S(2)}) collective-permute-start(bf16[2,1,192,320]{3,2,1,0:T(8,128)(2,1)} %slice_bitcast_fusion.12), channel_id=1, source_target_pairs={{0,1},{1,2},{2,3},{3,4},{4,5},{5,6},{6,7},{7,8},{8,9},{9,10},{10,1... | collective-permute-start | bytes 737288 | tf_op jit(solution)/shard_map/ppermute | solution.py:34
  101.1 9.6 %collective-permute-start.3 = (bf16[2,1,192,320]{3,2,1,0:T(8,128)(2,1)}, bf16[2,1,192,320]{3,2,1,0:T(8,128)(2,1)}, u32[]{:S(2)}, u32[]{:S(2)}) collective-permute-start(bf16[2,1,192,320]{3,2,1,0:T(8,128)(2,1)} %slice_bitcast_fusion.11), channel_id=1, source_target_pairs={{1,0},{2,1},{3,2},{4,3},{5,4},{6,5},{7,6},{8,7},{9,8},{10,9},{11,1... | collective-permute-start | bytes 737288 | tf_op jit(solution)/shard_map/ppermute | solution.py:35
  112.1 5.1 %slice-start = ((s8[4423680]{0:T(1024)(128)(4,1)}), s8[4194304]{0:T(1024)(128)(4,1)S(1)}, s32[]{:S(2)}) async-start(s8[4423680]{0:T(1024)(128)(4,1)} %bitcast.71), calls=%async_computation.4 | async-start | bytes 8388608
  116.7 0.9 slice-start.1
  117.0 0.7 copy-start.11
  125.4 1.5 copy-start.3
  126.9 1.7 %copy-start.5 = (bf16[1,2,6,192,320]{4,2,3,1,0:T(8,128)(2,1)S(1)}, bf16[1,2,6,192,320]{4,2,3,1,0:T(8,128)(2,1)}, u32[]{:S(2)}) copy-start(bf16[1,2,6,192,320]{4,2,3,1,0:T(8,128)(2,1)} %get-tuple-element.13) | copy-start | bytes 4423684
  130.6 10.3 %copy-start.1 = (bf16[4,6,192,320]{3,2,1,0:T(8,128)(2,1)S(1)}, bf16[4,6,192,320]{3,2,1,0:T(8,128)(2,1)}, u32[]{:S(2)}) copy-start(bf16[4,6,192,320]{3,2,1,0:T(8,128)(2,1)} %param.5) | copy-start | bytes 8847364
Sparse Core Ops, SparseCore 0:
  9.1 23.8 all-gather.4
where the time goes:
time: 150 us; the launch traced here: 148 us
  local copies, waits for them, and re-layouts  44.9 us (30%)
  starting transfers between devices  24.6 us (16%)
  other arithmetic  22.1 us (15%)
  matrix products  19.1 us (13%)
  blocking collectives  15.4 us (10%)
  between operations  13.8 us (9%)
  waiting for transfers between devices  7.89 us (5%)
    conv_general_dilated x2, matrix products, apply_layer(): lax.conv_general_dilated(normed, kernel, (1, 1), ((0, 0), (1, 1)), dimens...  19.1 us
    all_to_all x2, starting transfers between devices, sent_to_all(): return lax.all_to_all(copies, axis, split_axis=0, concat_axis=0, tiled=True)  15.3 us
    mul x2, local copies, waits for them, and re-layouts, group_moments(): values * values  10.2 us
    convert_element_type x2, other arithmetic, apply_layer(): normed = jnp.where(outside, 0.0, activated).astype(jnp.bfloat16)  8.89 us
    all_to_all x1, blocking collectives, on_device(): lax.all_to_all(stacked, 'section', split_axis=0, concat_axis=1, tiled=True)  8.51 us
    unnamed x30, local copies, waits for them, and re-layouts  7.69 us
    convert_element_type x2, local copies, waits for them, and re-layouts, group_moments(): inputs.astype(jnp.float32)  7.6 us
    ppermute x2, starting transfers between devices, padded_2(): before = lax.ppermute(last, axis, up)  6.76 us
  transfers between devices with their start and end apart: 7, of which 2 were waited for; matrix products, arithmetic and copies ran while one was open for 17% of the time, Pallas kernels for 0%

commit v1 on v0

v1 whole, which is shorter than its diff:
```python
import jax
import jax.numpy as jnp
from jax import lax
from jax.experimental import pallas as pl
from jax.experimental.pallas import tpu as pltpu
from jax.sharding import PartitionSpec as P

GROUPS = 32
EPS = 1e-5
F32 = jnp.float32
BF16 = jnp.bfloat16
MESH = pl.DeviceIdType.MESH
MAIN = 256
STEP = 16


def three_parts(row):
    high = row.astype(BF16)
    rest = row - high.astype(F32)
    middle = rest.astype(BF16)
    low = (rest - middle.astype(F32)).astype(BF16)
    return [high.astype(F32), middle.astype(F32), low.astype(F32)]


def stacked_parts(first, second):
    rows = three_parts(first) + three_parts(second)
    rows.append(jnp.zeros((10, first.shape[1]), F32))
    return jnp.concatenate(rows, axis=0).astype(BF16)


def make_kernel(n_space, samples, rows, columns, channels):
    half = rows // 2
    tail = channels - MAIN
    per_group = channels // GROUPS
    chunks = columns // STEP
    members = rows * n_space * columns * per_group
    peers = 2 * n_space

    def kernel(
        lat, ker, gain, bias, cbias, out,
        x_ref, w_ref, wt_ref, par_ref, f_ref, s_ref, y_ref, am_ref, pt_ref,
        g_ref, gt_ref, st0, st1, ab_ref,
        sem_x, sem_w, sem_p, sem_ws, sem_wr, sem_ps, sem_pr,
        sem_h0s, sem_h0r, sem_t0s, sem_t0r, sem_t1s, sem_t1r,
        sem_ds, sem_dr, sem_h1s, sem_h1r, sem_ol, sem_os, sem_or,
    ):
        space = lax.axis_index("space")
        sec = lax.axis_index("section")
        other = 1 - sec
        me = space * 2 + sec
        has_edge = jnp.logical_or(
            jnp.logical_and(sec == 0, space > 0),
            jnp.logical_and(sec == 1, space < n_space - 1),
        )
        beside = jnp.clip(space + 2 * sec - 1, 0, n_space - 1)
        partner = {"section": other}

        barrier = pltpu.get_barrier_semaphore()

        def greet(j, c):
            p = lax.rem(me + j, peers)
            pl.semaphore_signal(
                barrier, inc=1,
                device_id={"space": p // 2, "section": lax.rem(p, 2)},
                device_id_type=MESH,
            )
            return c

        lax.fori_loop(1, peers, greet, 0)

        def x_copy(b):
            return pltpu.make_async_copy(lat.at[b], x_ref.at[b, pl.ds(1, rows)], sem_x.at[b])

        small = (gain, bias, cbias)

        def p_copy(i):
            return pltpu.make_async_copy(small[i], par_ref.at[sec, i], sem_p.at[i])

        w_copy = pltpu.make_async_copy(ker.at[0], w_ref.at[sec], sem_w)
        for b in range(samples):
            x_copy(b).start()
        w_copy.start()
        for i in range(3):
            p_copy(i).start()

        shape = (channels, 128)
        low = lax.broadcasted_iota(jnp.int32, shape, 1) * per_group
        at = lax.broadcasted_iota(jnp.int32, shape, 0)
        g_ref[...] = jnp.where(jnp.logical_and(at >= low, at < low + per_group), 1.0, 0.0).astype(BF16)
        shape = (128, channels)
        low = lax.broadcasted_iota(jnp.int32, shape, 0) * per_group
        at = lax.broadcasted_iota(jnp.int32, shape, 1)
        gt_ref[...] = jnp.where(jnp.logical_and(at >= low, at < low + per_group), 1.0, 0.0).astype(BF16)

        pl.semaphore_wait(barrier, peers - 1)

        def h0_copy(b):
            return pltpu.make_async_remote_copy(
                lat.at[b, (rows - 1) * sec], x_ref.at[b, (rows + 1) * other],
                sem_h0s.at[b], sem_h0r.at[b],
                device_id={"space": beside, "section": other}, device_id_type=MESH,
            )

        w_send = pltpu.make_async_remote_copy(
            ker.at[0], w_ref.at[sec], sem_ws, sem_wr, device_id=partner, device_id_type=MESH
        )

        def p_send(i):
            return pltpu.make_async_remote_copy(
                small[i], par_ref.at[sec, i], sem_ps.at[i], sem_pr.at[i],
                device_id=partner, device_id_type=MESH,
            )

        @pl.when(has_edge)
        def _():
            for b in range(samples):
                h0_copy(b).start()

        for i in range(3):
            p_send(i).start()
        w_send.start()

        def group_sums(sums):
            s_m, s_t, q_m, q_t = [jnp.sum(v, axis=0, keepdims=True) for v in sums]
            total = jnp.zeros((16, 128), F32)
            for s, q, start, size in ((s_m, q_m, 0, MAIN), (s_t, q_t, MAIN, tail)):
                total += jnp.dot(
                    stacked_parts(s, q), g_ref[pl.ds(start, size), :], preferred_element_type=F32
                )
            return jnp.concatenate(
                [total[0:1] + total[1:2] + total[2:3], total[3:4] + total[4:5] + total[5:6]], axis=0
            )

        def folded(v):
            return v[0:8] + v[8:16]

        def zero_sums():
            return (
                jnp.zeros((8, MAIN), F32), jnp.zeros((8, tail), F32),
                jnp.zeros((8, MAIN), F32), jnp.zeros((8, tail), F32),
            )

        def added(sums, m, t):
            return (
                sums[0] + folded(m), sums[1] + folded(t),
                sums[2] + folded(m * m), sums[3] + folded(t * t),
            )

        def t0_send(b, j):
            return pltpu.make_async_remote_copy(
                st0.at[b, space], st0.at[b, space], sem_t0s.at[b], sem_t0r.at[b],
                device_id={"space": lax.rem(space + j, n_space)}, device_id_type=MESH,
            )

        def input_stats(b, c):
            x_copy(b).wait()

            def row(r, sums):
                for k in range(chunks):
                    at = pl.ds(k * STEP, STEP)
                    m = x_ref[b, r, at, 0:MAIN].astype(F32)
                    t = x_ref[b, r, at, MAIN:channels].astype(F32)
                    sums = added(sums, m, t)
                return sums

            st0[b, space] = group_sums(lax.fori_loop(1, rows + 1, row, zero_sums()))

            def send(j, c):
                t0_send(b, j).start()
                return c

            lax.fori_loop(1, n_space, send, 0)
            return c

        lax.fori_loop(0, samples, input_stats, 0)

        def affine(layer, totals):
            mean = totals[0:1] * (1.0 / members)
            var = jnp.maximum(totals[1:2] * (1.0 / members) - mean * mean, 0.0)
            inv = lax.rsqrt(var + EPS)
            parts = stacked_parts(inv, mean * inv)
            spread = jnp.dot(parts, gt_ref[...], preferred_element_type=F32)
            inv_c = spread[0:1] + spread[1:2] + spread[2:3]
            shift_c = spread[3:4] + spread[4:5] + spread[5:6]
            g = par_ref[layer, 0]
            ab_ref[0:1, :] = inv_c * g * 0.5
            ab_ref[1:2, :] = (par_ref[layer, 1] - shift_c * g) * 0.5

        def norm_row(src, dst):
            a_m, a_t = ab_ref[0:1, 0:MAIN], ab_ref[0:1, MAIN:channels]
            b_m, b_t = ab_ref[1:2, 0:MAIN], ab_ref[1:2, MAIN:channels]

            def act(k):
                at = pl.ds(k * STEP, STEP)
                h = src[at, 0:MAIN].astype(F32) * a_m + b_m
                m = h + h * jnp.tanh(h)
                h = src[at, MAIN:channels].astype(F32) * a_t + b_t
                return m, h + h * jnp.tanh(h)

            none = (jnp.zeros((8, MAIN), F32), jnp.zeros((8, tail), F32))
            before, now = none, act(0)
            zeros = jnp.zeros((STEP, 256 - 3 * tail), F32)
            for k in range(chunks):
                later = act(k + 1) if k < chunks - 1 else None
                head = none if later is None else (later[0][0:8], later[1][0:8])
                wide = [jnp.concatenate([p, n, h], axis=0) for p, n, h in zip(before, now, head)]
                at = pl.ds(k * STEP, STEP)
                dst[at, 0:256] = wide[0][7:23].astype(BF16)
                dst[at, 256:512] = now[0].astype(BF16)
                dst[at, 512:768] = wide[0][9:25].astype(BF16)
                dst[at, 768:1024] = jnp.concatenate(
                    [wide[1][7:23], now[1], wide[1][9:25], zeros], axis=1
                ).astype(BF16)
                before, now = (now[0][8:16], now[1][8:16]), later

        def norm_all(src_of):
            def row(j, c):
                i = j + 1 - sec
                norm_row(src_of(i), y_ref.at[i])
                return c

            lax.fori_loop(0, half + 1, row, 0)
            edge = (half + 1) * sec

            @pl.when(has_edge)
            def _():
                norm_row(src_of(edge), y_ref.at[edge])

            @pl.when(jnp.logical_not(has_edge))
            def _():
                y_ref[edge] = jnp.zeros((columns, 1024), BF16)

        def pack_tail(layer):
            for dc in range(3):
                taps = [w_ref[layer, dr, dc, :, MAIN:channels].astype(F32) for dr in range(3)]
                taps.append(jnp.zeros((channels, 256 - 3 * tail), F32))
                packed = jnp.concatenate(taps, axis=1).astype(BF16)
                wt_ref[pl.ds(dc * MAIN, MAIN), :] = packed[0:MAIN]
                wt_ref[pl.ds(3 * MAIN + dc * tail, tail), :] = packed[MAIN:channels]
            wt_ref[pl.ds(3 * MAIN + 3 * tail, 256 - 3 * tail), :] = jnp.zeros((256 - 3 * tail, 256), BF16)

        def convolve(layer):
            pieces = []
            for dr in range(3):
                tiles = [w_ref[layer, dr, dc, 0:MAIN, 0:MAIN] for dc in range(3)]
                tiles += [w_ref[layer, dr, dc, MAIN:channels, 0:MAIN] for dc in range(3)]
                tiles.append(jnp.zeros((256 - 3 * tail, MAIN), BF16))
                pieces.append(jnp.concatenate(tiles, axis=0))
            for r in range(half):
                acc = None
                for dr in range(3):
                    part = jnp.dot(y_ref[r + dr], pieces[dr], preferred_element_type=F32)
                    acc = part if acc is None else acc + part
                am_ref[r] = acc
            for i in range(half + 2):
                pt_ref[i] = jnp.dot(y_ref[i], wt_ref[...], preferred_element_type=F32)

        def conv_out(r, at):
            m = am_ref[r, at, :]
            t = (
                pt_ref[r, at, 0:tail]
                + pltpu.roll(pt_ref[r + 1, at, 0:128], 64, 1)[:, 0:tail]
                + pt_ref[r + 2, at, 128 : 128 + tail]
            )
            return m, t

        def out_move(layer, b, ref):
            span = pl.ds(half * sec, half)
            local = pltpu.make_async_copy(ref, out.at[0, b, span], sem_ol.at[b])
            remote = pltpu.make_async_remote_copy(
                ref, out.at[0, b, span], sem_os.at[b], sem_or.at[b],
                device_id=partner, device_id_type=MESH,
            )
            return local, remote

        def first_view(b):
            return f_ref.at[b, pl.ds(1, half)]

        def out_start(layer, b, ref):
            local, remote = out_move(layer, b, ref)

            @pl.when(sec == layer)
            def _():
                local.start()

            @pl.when(sec != layer)
            def _():
                remote.start()

        def t1_send(b, j):
            p = lax.rem(me + j, peers)
            return pltpu.make_async_remote_copy(
                st1.at[b, me], st1.at[b, me], sem_t1s.at[b], sem_t1r.at[b],
                device_id={"space": p // 2, "section": lax.rem(p, 2)}, device_id_type=MESH,
            )

        def d_send(b):
            return pltpu.make_async_remote_copy(
                f_ref.at[b, half - (half - 1) * sec], f_ref.at[b, (half + 1) * sec],
                sem_ds.at[b], sem_dr.at[b], device_id=partner, device_id_type=MESH,
            )

        def h1_send(b):
            return pltpu.make_async_remote_copy(
                f_ref.at[b, 1 + (half - 1) * sec], f_ref.at[b, (half + 1) * other],
                sem_h1s.at[b], sem_h1r.at[b],
                device_id={"space": beside, "section": other}, device_id_type=MESH,
            )

        def all_bytes(ref, b, count, sem):
            view = ref.at[b, pl.ds(0, count)]
            return pltpu.make_async_copy(view, view, sem.at[b])

        w_copy.wait()
        for i in range(3):
            p_copy(i).wait()
        for i in range(3):
            p_send(i).wait()
        w_send.wait()

        pack_tail(0)

        def first_stage(b, c):
            @pl.when(has_edge)
            def _():
                h0_copy(b).wait_recv()

            all_bytes(st0, b, n_space - 1, sem_t0r).wait()
            affine(0, jnp.sum(st0[b], axis=0))
            base = half * sec
            norm_all(lambda i: x_ref.at[b, base + i])
            convolve(0)
            cb = par_ref[0, 2]

            def row(r, sums):
                for k in range(chunks):
                    at = pl.ds(k * STEP, STEP)
                    m, t = conv_out(r, at)
                    m = (m + cb[:, 0:MAIN]).astype(BF16)
                    t = (t + cb[:, MAIN:channels]).astype(BF16)
                    f_ref[b, 1 + r, at, 0:MAIN] = m
                    f_ref[b, 1 + r, at, MAIN:channels] = t
                    sums = added(sums, m.astype(F32), t.astype(F32))
                return sums

            sums = lax.fori_loop(0, half, row, zero_sums())
            st1[b, me] = group_sums(sums)

            def send(j, c):
                t1_send(b, j).start()
                return c

            lax.fori_loop(1, peers, send, 0)
            d_send(b).start()

            @pl.when(has_edge)
            def _():
                h1_send(b).start()

            out_start(0, b, first_view(b))
            return c

        lax.fori_loop(0, samples, first_stage, 0)

        pack_tail(1)

        def second_stage(b, c):
            d_send(b).wait_recv()

            @pl.when(has_edge)
            def _():
                h1_send(b).wait_recv()

            all_bytes(st1, b, peers - 1, sem_t1r).wait()
            affine(1, jnp.sum(st1[b], axis=0))
            norm_all(lambda i: f_ref.at[b, i])
            convolve(1)
            cb = par_ref[1, 2]

            def row(r, c):
                for k in range(chunks):
                    at = pl.ds(k * STEP, STEP)
                    m, t = conv_out(r, at)
                    xr = x_ref.at[b, 1 + half * sec + r]
                    m = m + xr[at, 0:MAIN].astype(F32) + cb[:, 0:MAIN]
                    t = t + xr[at, MAIN:channels].astype(F32) + cb[:, MAIN:channels]
                    s_ref[b, r, at, 0:MAIN] = m.astype(BF16)
                    s_ref[b, r, at, MAIN:channels] = t.astype(BF16)
                return c

            lax.fori_loop(0, half, row, 0)

            out_start(1, b, s_ref.at[b])
            return c

        lax.fori_loop(0, samples, second_stage, 0)

        def finish(b, c):
            @pl.when(has_edge)
            def _():
                h0_copy(b).wait_send()
                h1_send(b).wait_send()

            all_bytes(st0, b, n_space - 1, sem_t0s).wait()
            all_bytes(st1, b, peers - 1, sem_t1s).wait()
            d_send(b).wait_send()
            local, remote = out_move(0, b, first_view(b))
            local.wait()
            remote.wait_send()
            remote.wait_recv()
            return c

        lax.fori_loop(0, samples, finish, 0)

    dma = pltpu.SemaphoreType.DMA
    per_sample = dma((samples,))
    scratch = [
        pltpu.VMEM((samples, rows + 2, columns, channels), BF16),
        pltpu.VMEM((2, 3, 3, channels, channels), BF16),
        pltpu.VMEM((1024, 256), BF16),
        pltpu.VMEM((2, 3, 1, channels), F32),
        pltpu.VMEM((samples, half + 2, columns, channels), BF16),
        pltpu.VMEM((samples, half, columns, channels), BF16),
        pltpu.VMEM((half + 2, columns, 1024), BF16),
        pltpu.VMEM((half, columns, MAIN), F32),
        pltpu.VMEM((half + 2, columns, 256), F32),
        pltpu.VMEM((channels, 128), BF16),
        pltpu.VMEM((128, channels), BF16),
        pltpu.VMEM((samples, n_space, 2, 128), F32),
        pltpu.VMEM((samples, peers, 2, 128), F32),
        pltpu.VMEM((8, channels), F32),
        per_sample, dma, dma((3,)), dma, dma, dma((3,)), dma((3,)),
        per_sample, per_sample, per_sample, per_sample, per_sample, per_sample,
        per_sample, per_sample, per_sample, per_sample, per_sample, per_sample, per_sample,
    ]
    return kernel, scratch


def solution(mesh):
    n_space = mesh.shape["space"]

    def on_device(latents, kernels, norm_gain, norm_bias, conv_bias):
        samples, rows, columns, channels = latents.shape
        kernel, scratch = make_kernel(n_space, samples, rows, columns, channels)
        return pl.pallas_call(
            kernel,
            out_shape=jax.ShapeDtypeStruct((1, samples, rows, columns, channels), BF16),
            in_specs=[pl.BlockSpec(memory_space=pl.ANY)] * 5,
            out_specs=pl.BlockSpec(memory_space=pl.ANY),
            scratch_shapes=scratch,
            compiler_params=pltpu.CompilerParams(
                collective_id=0, has_side_effects=True, vmem_limit_bytes=56 * 1024 * 1024
            ),
            name="resblock",
        )(latents, kernels, norm_gain, norm_bias, conv_bias)

    return jax.shard_map(
        on_device,
        mesh=mesh,
        in_specs=(
            P("dp", "space", None, None),
            P("section", None, None, None, None),
            P("section", None),
            P("section", None),
            P("section", None),
        ),
        out_specs=P("section", "dp", "space", None, None),
        check_vma=False,
    )
```

time: 150 us -> 50.3 us (0.34); the launches traced: 148 us -> 50 us
  Pallas kernels: 0 us -> 45.8 us
  local copies, waits for them, and re-layouts: 44.9 us -> 4.21 us
  starting transfers between devices: 24.6 us -> 0 us
  other arithmetic: 22.1 us -> 0 us
  matrix products: 19.1 us -> 0 us
  blocking collectives: 15.4 us -> 0 us
  between operations: 13.8 us -> 0.01 us
  waiting for transfers between devices: 7.89 us -> 0 us
    pallas_call x0 -> x1, Pallas kernels: none -> 45.8 us  [on_device(): pl.pallas_call(kernel, out_shape=jax.ShapeDtypeStruct((1, samples, rows,...]
    conv_general_dilated x2 -> x0, matrix products: 19.1 us -> none  [apply_layer(): lax.conv_general_dilated(normed, kernel, (1, 1), ((0, 0), (1, 1)), dimens...]
    all_to_all x2 -> x0, starting transfers between devices: 15.3 us -> none  [sent_to_all(): return lax.all_to_all(copies, axis, split_axis=0, concat_axis=0, tiled=True)]
    mul x6 -> x0, local copies, waits for them, and re-layouts: 10.6 us -> none  [the longest x2 10.2 us: group_moments(): values * values]
    convert_element_type x10 -> x0, local copies, waits for them, and re-layouts: 10.6 us -> none  [the longest x2 7.6 us: group_moments(): inputs.astype(jnp.float32)]
    ppermute x4 -> x0, starting transfers between devices: 9.34 us -> none  [the longest x2 6.76 us: padded_2(): before = lax.ppermute(last, axis, up)]
    convert_element_type x5 -> x0, other arithmetic: 8.9 us -> none  [the longest x2 8.89 us: apply_layer(): normed = jnp.where(outside, 0.0, activated).astype(jnp.bfloat16)]
    all_to_all x1 -> x0, blocking collectives: 8.51 us -> none  [on_device(): lax.all_to_all(stacked, 'section', split_axis=0, concat_axis=1, tiled=True)]
  transfers between devices with their start and end apart: 7 -> 0, of which waited for: 2 -> 0; matrix products, arithmetic and copies ran while one was open for 17% -> 0% of each run, Pallas kernels for 0% -> 0%
where the time goes in v1:
time: 50.3 us; the launch traced here: 50 us
  Pallas kernels  45.8 us (91%)
  local copies, waits for them, and re-layouts  4.21 us (8%)
    pallas_call x1, Pallas kernels, on_device(): pl.pallas_call(kernel, out_shape=jax.ShapeDtypeStruct((1, samples, rows,...  45.8 us
    unnamed x1, local copies, waits for them, and re-layouts  4.21 us

profile of v1, /device:TPU:1, one launch (start us, length us, event | category | flops | bytes accessed | tf_op | source)
XLA Modules:
  0.0 50.0 jit_solution(18119969626667164188)
XLA Ops:
  0.0 45.8 %resblock.1 = bf16[1,4,6,192,320]{4,3,2,1,0:T(8,128)(2,1)} custom-call(bf16[4,6,192,320]{3,2,1,0:T(8,128)(2,1)} %lat.1, bf16[1,3,3,320,320]{4,3,2,1,0:T(8,128)(2,1)} %ker.1, f32[1,320]{1,0:T(1,128)} %gain.1, f32[1,320]{1,0:T(1,128)} %bias.1, f32[1,320]{1,0:T(1,128)} %cbias.1), custom_call_target="tpu_custom_call" | custom-call | tf_op jit(solution)/shard_map/resblock/pallas_call | solution.py:445
  45.8 4.2 %copy.7 = bf16[1,4,6,192,320]{4,3,2,1,0:T(8,128)(2,1)} copy(bf16[1,4,6,192,320]{4,3,2,1,0:T(8,128)(2,1)} %resblock.1) | data formatting | bytes 5898240

commit v2 on v1

v2 whole, which is shorter than its diff:
```python
import jax
import jax.numpy as jnp
from jax import lax
from jax.experimental import pallas as pl
from jax.experimental.pallas import tpu as pltpu
from jax.sharding import PartitionSpec as P

GROUPS = 32
EPS = 1e-5
F32 = jnp.float32
BF16 = jnp.bfloat16
MESH = pl.DeviceIdType.MESH
MAIN = 256
STEP = 16


def three_parts(row):
    high = row.astype(BF16)
    rest = row - high.astype(F32)
    middle = rest.astype(BF16)
    low = (rest - middle.astype(F32)).astype(BF16)
    return [high.astype(F32), middle.astype(F32), low.astype(F32)]


def stacked_parts(first, second):
    rows = three_parts(first) + three_parts(second)
    rows.append(jnp.zeros((10, first.shape[1]), F32))
    return jnp.concatenate(rows, axis=0).astype(BF16)


def make_kernel(n_space, samples, rows, columns, channels):
    half = rows // 2
    tail = channels - MAIN
    per_group = channels // GROUPS
    chunks = columns // STEP
    members = rows * n_space * columns * per_group
    peers = 2 * n_space
    stages = 2 * samples

    def kernel(
        lat, ker, gain, bias, cbias, out,
        x_ref, w_ref, wt_ref, par_ref, f_ref, s_ref, ya_ref, yb_ref, ta_ref, tb_ref, am_ref, pt_ref,
        g_ref, gt_ref, st_ref,
        sem_x, sem_w, sem_p, sem_ws, sem_wr, sem_ps, sem_pr,
        sem_hs, sem_hr, sem_ts, sem_tr, sem_ds, sem_dr, sem_ol, sem_os, sem_or,
    ):
        space = lax.axis_index("space")
        sec = lax.axis_index("section")
        other = 1 - sec
        me = space * 2 + sec
        at_top = jnp.logical_and(sec == 0, space == 0)
        at_bottom = jnp.logical_and(sec == 1, space == n_space - 1)
        has_edge = jnp.logical_not(jnp.logical_or(at_top, at_bottom))
        beside = jnp.clip(space + 2 * sec - 1, 0, n_space - 1)
        partner = {"section": other}

        barrier = pltpu.get_barrier_semaphore()

        def everyone():
            for j in range(n_space):
                there = lax.rem(space + j, n_space) if j else space
                for t in (0, 1):
                    if j or t:
                        yield {"space": there, "section": other if t else sec}

        for peer in everyone():
            pl.semaphore_signal(barrier, inc=1, device_id=peer, device_id_type=MESH)

        def x_copy(b):
            return pltpu.make_async_copy(
                lat.at[b, pl.ds((half - 1) * sec, half + 1)],
                x_ref.at[b, pl.ds(other, half + 1)], sem_x.at[b],
            )

        small = (gain, bias, cbias)

        def p_copy(i):
            return pltpu.make_async_copy(small[i], par_ref.at[sec, i], sem_p.at[i])

        w_copy = pltpu.make_async_copy(ker.at[0], w_ref.at[sec], sem_w)
        for b in range(samples):
            x_copy(b).start()
        w_copy.start()
        for i in range(3):
            p_copy(i).start()

        shape = (channels, 128)
        low = lax.broadcasted_iota(jnp.int32, shape, 1) * per_group
        at = lax.broadcasted_iota(jnp.int32, shape, 0)
        g_ref[...] = jnp.where(jnp.logical_and(at >= low, at < low + per_group), 1.0, 0.0).astype(BF16)
        shape = (128, channels)
        low = lax.broadcasted_iota(jnp.int32, shape, 0) * per_group
        at = lax.broadcasted_iota(jnp.int32, shape, 1)
        gt_ref[...] = jnp.where(jnp.logical_and(at >= low, at < low + per_group), 1.0, 0.0).astype(BF16)
        pt_ref[...] = jnp.zeros_like(pt_ref)
        ta_ref[...] = jnp.zeros_like(ta_ref)
        tb_ref[...] = jnp.zeros_like(tb_ref)

        @pl.when(jnp.logical_not(has_edge))
        def _():
            def clear(b, c):
                x_ref[b, (half + 1) * sec] = jnp.zeros((columns, channels), BF16)
                f_ref[b, (half + 1) * sec] = jnp.zeros((columns, channels), BF16)
                return c

            lax.fori_loop(0, samples, clear, 0)

        def group_sums(sums):
            s_m, s_t, q_m, q_t = [jnp.sum(v, axis=0, keepdims=True) for v in sums]
            total = jnp.zeros((16, 128), F32)
            for s, q, start, size in ((s_m, q_m, 0, MAIN), (s_t, q_t, MAIN, tail)):
                total += jnp.dot(
                    stacked_parts(s, q), g_ref[pl.ds(start, size), :], preferred_element_type=F32
                )
            return jnp.concatenate(
                [total[0:1] + total[1:2] + total[2:3], total[3:4] + total[4:5] + total[5:6]], axis=0
            )

        def folded(v):
            return v[0:8] + v[8:16]

        def zero_sums():
            return (
                jnp.zeros((8, MAIN), F32), jnp.zeros((8, tail), F32),
                jnp.zeros((8, MAIN), F32), jnp.zeros((8, tail), F32),
            )

        def added(sums, m, t):
            return (
                sums[0] + folded(m), sums[1] + folded(t),
                sums[2] + folded(m * m), sums[3] + folded(t * t),
            )

        def input_stats(b, c):
            x_copy(b).wait()

            def row(r, sums):
                for k in range(chunks):
                    at = pl.ds(k * STEP, STEP)
                    m = x_ref[b, r, at, 0:MAIN].astype(F32)
                    t = x_ref[b, r, at, MAIN:channels].astype(F32)
                    sums = added(sums, m, t)
                return sums

            st_ref[b, me] = group_sums(lax.fori_loop(1, half + 1, row, zero_sums()))
            return c

        lax.fori_loop(0, samples, input_stats, 0)

        def pack_tail(layer):
            for dr in range(3):
                taps = [w_ref[layer, dr, dc, :, MAIN:channels].astype(F32) for dc in range(3)]
                taps.append(jnp.zeros((channels, 256 - 3 * tail), F32))
                packed = jnp.concatenate(taps, axis=1).astype(BF16)
                wt_ref[layer, pl.ds(dr * MAIN, MAIN), :] = packed[0:MAIN]
                wt_ref[layer, pl.ds(3 * MAIN + dr * tail, tail), :] = packed[MAIN:channels]
            wt_ref[layer, pl.ds(3 * MAIN + 3 * tail, 256 - 3 * tail), :] = jnp.zeros(
                (256 - 3 * tail, 256), BF16
            )

        w_copy.wait()
        for i in range(3):
            p_copy(i).wait()
        pack_tail(sec)

        pl.semaphore_wait(barrier, peers - 1)

        def t_sends(k):
            return [
                pltpu.make_async_remote_copy(
                    st_ref.at[k, me], st_ref.at[k, me], sem_ts.at[k], sem_tr.at[k],
                    device_id=peer, device_id_type=MESH,
                )
                for peer in everyone()
            ]

        def halo(k):
            ref = x_ref if k < samples else f_ref
            b = k % samples
            return pltpu.make_async_remote_copy(
                ref.at[b, 1 + (half - 1) * sec], ref.at[b, (half + 1) * other],
                sem_hs.at[k], sem_hr.at[k],
                device_id={"space": beside, "section": other}, device_id_type=MESH,
            )

        w_send = pltpu.make_async_remote_copy(
            w_ref.at[sec], w_ref.at[sec], sem_ws, sem_wr, device_id=partner, device_id_type=MESH
        )

        def p_send(i):
            return pltpu.make_async_remote_copy(
                par_ref.at[sec, i], par_ref.at[sec, i], sem_ps.at[i], sem_pr.at[i],
                device_id=partner, device_id_type=MESH,
            )

        for i in range(3):
            p_send(i).start()
        w_send.start()
        for k in range(samples):
            for copy in t_sends(k):
                copy.start()

            @pl.when(has_edge)
            def _(k=k):
                halo(k).start()

        def affine(k):
            layer = k // samples
            totals = jnp.sum(st_ref[k], axis=0)
            mean = totals[0:1] * (1.0 / members)
            var = jnp.maximum(totals[1:2] * (1.0 / members) - mean * mean, 0.0)
            inv = lax.rsqrt(var + EPS)
            spread = jnp.dot(
                stacked_parts(inv, mean * inv), gt_ref[...], preferred_element_type=F32
            )
            inv_c = spread[0:1] + spread[1:2] + spread[2:3]
            shift_c = spread[3:4] + spread[4:5] + spread[5:6]
            g = par_ref[layer, 0]
            a = inv_c * g * 0.5
            return a, (par_ref[layer, 1] - shift_c * g) * 0.5

        top_keep = jnp.where(at_top, 0.0, 1.0)
        bottom_keep = jnp.where(at_bottom, 0.0, 1.0)

        def norm_row(k, i, ab, y, t):
            ref = x_ref if k < samples else f_ref
            b = k % samples
            a, s = ab
            if i == 0:
                a, s = a * top_keep, s * top_keep
            if i == half + 1:
                a, s = a * bottom_keep, s * bottom_keep
            a_m, a_t, b_m, b_t = a[:, 0:MAIN], a[:, MAIN:], s[:, 0:MAIN], s[:, MAIN:]

            def act(c):
                at = pl.ds(c * STEP, STEP)
                h = ref[b, i, at, 0:MAIN].astype(F32) * a_m + b_m
                m = h + h * jnp.tanh(h)
                h = ref[b, i, at, MAIN:channels].astype(F32) * a_t + b_t
                return m, h + h * jnp.tanh(h)

            none = (jnp.zeros((8, MAIN), F32), jnp.zeros((8, tail), F32))
            before, now = none, act(0)
            zeros = jnp.zeros((STEP, 256 - 3 * tail), F32)
            for c in range(chunks):
                later = act(c + 1) if c < chunks - 1 else None
                after = none if later is None else (later[0][0:8], later[1][0:8])
                wide = [jnp.concatenate([p, n, h], axis=0) for p, n, h in zip(before, now, after)]
                at = pl.ds(c * STEP, STEP)
                y[i, at, 0:256] = wide[0][7:23].astype(BF16)
                y[i, at, 256:512] = now[0].astype(BF16)
                y[i, at, 512:768] = wide[0][9:25].astype(BF16)
                packed = jnp.concatenate(
                    [wide[1][7:23], now[1], wide[1][9:25], zeros], axis=1
                ).astype(BF16)
                y[i, at, 768:1024] = packed
                own = now[1].astype(BF16)
                if i < half:
                    t[i, at, 0:tail] = own
                if 1 <= i <= half:
                    t[i - 1, at, tail : 2 * tail] = packed[:, tail : 2 * tail]
                if i >= 2:
                    t[i - 2, at, 2 * tail : 3 * tail] = own
                before, now = (now[0][8:16], now[1][8:16]), later

        def stage(k):
            layer, b = k // samples, k % samples
            y, t = ((ya_ref, ta_ref), (yb_ref, tb_ref))[k % 2]
            y_next, t_next = ((yb_ref, tb_ref), (ya_ref, ta_ref))[k % 2]
            more = k + 1 < stages
            if more:
                ab = affine(k + 1)
            for r in range(half):
                lhs = jnp.concatenate([y[r + dr, :, 256:512] for dr in range(3)] + [t[r]], axis=1)
                pt_ref[r, pl.ds(8, columns), :] = jnp.dot(
                    lhs, wt_ref[layer], preferred_element_type=F32
                )
            tiles = []
            for dr in range(3):
                tiles += [w_ref[layer, dr, dc, 0:MAIN, 0:MAIN] for dc in range(3)]
                tiles += [w_ref[layer, dr, dc, MAIN:channels, 0:MAIN] for dc in range(3)]
                tiles.append(jnp.zeros((256 - 3 * tail, MAIN), BF16))
            weights = jnp.concatenate(tiles, axis=0)
            cb = par_ref[layer, 2]
            sums = zero_sums()
            norms = list(range(half + 2))
            for r in range(half):
                lhs = jnp.concatenate([y[r + dr] for dr in range(3)], axis=1)
                am_ref[r] = jnp.dot(lhs, weights, preferred_element_type=F32)
                if more:
                    for i in norms[2 * r : 2 * r + 2]:
                        norm_row(k + 1, i, ab, y_next, t_next)
            for r in range(half):
                for c in range(chunks):
                    at = pl.ds(c * STEP, STEP)
                    m = am_ref[r, at, :] + cb[:, 0:MAIN]
                    wide = pt_ref[r, pl.ds(c * STEP, STEP + 16), :]
                    u = (
                        wide[7:23, 0:tail]
                        + pltpu.roll(wide[8:24, 0:128], 64, 1)[:, 0:tail]
                        + wide[9:25, 128 : 128 + tail]
                        + cb[:, MAIN:channels]
                    )
                    if layer == 0:
                        m, u = m.astype(BF16), u.astype(BF16)
                        f_ref[b, 1 + r, at, 0:MAIN] = m
                        f_ref[b, 1 + r, at, MAIN:channels] = u
                        sums = added(sums, m.astype(F32), u.astype(F32))
                    else:
                        m = m + x_ref[b, 1 + r, at, 0:MAIN].astype(F32)
                        u = u + x_ref[b, 1 + r, at, MAIN:channels].astype(F32)
                        s_ref[b, r, at, 0:MAIN] = m.astype(BF16)
                        s_ref[b, r, at, MAIN:channels] = u.astype(BF16)
            if layer == 0:
                st_ref[k + samples, me] = group_sums(sums)

        def out_move(layer, b):
            ref = f_ref.at[b, pl.ds(1, half)] if layer == 0 else s_ref.at[b]
            span = pl.ds(half * sec, half)
            local = pltpu.make_async_copy(ref, out.at[0, b, span], sem_ol.at[b])
            remote = pltpu.make_async_remote_copy(
                ref, out.at[0, b, span], sem_os.at[b], sem_or.at[b],
                device_id=partner, device_id_type=MESH,
            )
            return local, remote

        def out_start(layer, b):
            local, remote = out_move(layer, b)

            @pl.when(sec == layer)
            def _():
                local.start()

            @pl.when(sec != layer)
            def _():
                remote.start()

        def d_send(b):
            return pltpu.make_async_remote_copy(
                f_ref.at[b, half - (half - 1) * sec], f_ref.at[b, (half + 1) * sec],
                sem_ds.at[b], sem_dr.at[b], device_id=partner, device_id_type=MESH,
            )

        def all_bytes(k, sem):
            view = st_ref.at[k, pl.ds(0, peers - 1)]
            return pltpu.make_async_copy(view, view, sem.at[k])

        def arrived(k):
            if k >= samples:
                d_send(k - samples).wait_recv()

            @pl.when(has_edge)
            def _():
                halo(k).wait_recv()

            all_bytes(k, sem_tr).wait()

        for i in range(3):
            p_send(i).wait()
        arrived(0)
        ab = affine(0)
        for i in range(half + 2):
            norm_row(0, i, ab, ya_ref, ta_ref)
        w_send.wait()
        pack_tail(other)

        for k in range(stages):
            if k + 1 < stages:
                arrived(k + 1)
            stage(k)
            layer, b = k // samples, k % samples
            if layer == 0:
                for copy in t_sends(k + samples):
                    copy.start()
                d_send(b).start()

                @pl.when(has_edge)
                def _(k=k):
                    halo(k + samples).start()

            out_start(layer, b)

        for k in range(stages):
            @pl.when(has_edge)
            def _(k=k):
                halo(k).wait_send()

            all_bytes(k, sem_ts).wait()
        for b in range(samples):
            d_send(b).wait_send()
            local, remote = out_move(0, b)
            local.wait()
            remote.wait_send()
            remote.wait_recv()

    dma = pltpu.SemaphoreType.DMA
    each, both = dma((samples,)), dma((2 * samples,))
    scratch = [
        pltpu.VMEM((samples, half + 2, columns, channels), BF16),
        pltpu.VMEM((2, 3, 3, channels, channels), BF16),
        pltpu.VMEM((2, 1024, 256), BF16),
        pltpu.VMEM((2, 3, 1, channels), F32),
        pltpu.VMEM((samples, half + 2, columns, channels), BF16),
        pltpu.VMEM((samples, half, columns, channels), BF16),
        pltpu.VMEM((half + 2, columns, 1024), BF16),
        pltpu.VMEM((half + 2, columns, 1024), BF16),
        pltpu.VMEM((half, columns, 256), BF16),
        pltpu.VMEM((half, columns, 256), BF16),
        pltpu.VMEM((half, columns, MAIN), F32),
        pltpu.VMEM((half, columns + 16, 256), F32),
        pltpu.VMEM((channels, 128), BF16),
        pltpu.VMEM((128, channels), BF16),
        pltpu.VMEM((2 * samples, peers, 2, 128), F32),
        each, dma, dma((3,)), dma, dma, dma((3,)), dma((3,)),
        both, both, both, both, each, each, each, each, each,
    ]
    return kernel, scratch


def solution(mesh):
    n_space = mesh.shape["space"]

    def on_device(latents, kernels, norm_gain, norm_bias, conv_bias):
        samples, rows, columns, channels = latents.shape
        kernel, scratch = make_kernel(n_space, samples, rows, columns, channels)
        return pl.pallas_call(
            kernel,
            out_shape=pltpu.VMEM((1, samples, rows, columns, channels), BF16),
            in_specs=[pl.BlockSpec(memory_space=pl.ANY)] * 5,
            out_specs=pl.BlockSpec(memory_space=pltpu.VMEM),
            scratch_shapes=scratch,
            compiler_params=pltpu.CompilerParams(
                collective_id=0, has_side_effects=True, vmem_limit_bytes=56 * 1024 * 1024
            ),
            name="resblock",
        )(latents, kernels, norm_gain, norm_bias, conv_bias)

    return jax.shard_map(
        on_device,
        mesh=mesh,
        in_specs=(
            P("dp", "space", None, None),
            P("section", None, None, None, None),
            P("section", None),
            P("section", None),
            P("section", None),
        ),
        out_specs=P("section", "dp", "space", None, None),
        check_vma=False,
    )
```

time: 50.3 us -> 38.1 us (0.76)
  Pallas kernels: 45.8 us -> 36.2 us
  local copies, waits for them, and re-layouts: 4.21 us -> 1.8 us
    pallas_call x1, Pallas kernels: 45.8 us -> 36.2 us  [on_device(): pl.pallas_call(kernel, out_shape=pltpu.VMEM((1, samples, rows, columns, c...]
    unnamed x1, local copies, waits for them, and re-layouts: 4.21 us -> 1.8 us
where the time goes in v2:
time: 38.1 us; the launch traced here: 38 us
  Pallas kernels  36.2 us (95%)
  local copies, waits for them, and re-layouts  1.8 us (5%)
    pallas_call x1, Pallas kernels, on_device(): pl.pallas_call(kernel, out_shape=pltpu.VMEM((1, samples, rows, columns, c...  36.2 us
    unnamed x1, local copies, waits for them, and re-layouts  1.8 us

profile of v2, /device:TPU:1, one launch (start us, length us, event | category | flops | bytes accessed | tf_op | source)
XLA Modules:
  0.0 38.0 jit_solution(12645715214169382788)
XLA Ops:
  0.0 36.2 %resblock.1 = bf16[1,4,6,192,320]{4,3,2,1,0:T(8,128)(2,1)S(1)} custom-call(bf16[4,6,192,320]{3,2,1,0:T(8,128)(2,1)} %lat.1, bf16[1,3,3,320,320]{4,3,2,1,0:T(8,128)(2,1)} %ker.1, f32[1,320]{1,0:T(1,128)} %gain.1, f32[1,320]{1,0:T(1,128)} %bias.1, f32[1,320]{1,0:T(1,128)} %cbias.1), custom_call_target="tpu_custom_call" | custom-call | tf_op jit(solution)/shard_map/resblock/pallas_call | solution.py:426
  36.2 1.8 %copy.7 = bf16[1,4,6,192,320]{4,3,2,1,0:T(8,128)(2,1)} copy(bf16[1,4,6,192,320]{4,3,2,1,0:T(8,128)(2,1)S(1)} %resblock.1) | data formatting | bytes 5898240
